TPU v7x, 128 devices: a whole 4x4x4 slice. The times are simulated.
128 devices in a mesh: chan: 8 (over x, core), tile: 16 (over z, y).
Axes of the slice: x: 4, y: 4, z: 4, core: 2. Of those that a mesh axis runs over, the one named last changes fastest.
Arguments:
- voltages: bfloat16 [8, 2, 2048, 2048], P(None, None, 'tile', 'chan'), may hold values from -16 to 16
- rfi_flags: int32 [8], P('chan'), may hold values 0 or 1
- beam_steer_index: int32 [8, 8], P('chan'), may hold values from 0 to 2047
- start_columns: int32 [8, 32], P('chan'), may hold values from 0 to 2047, as said below
Outputs:
- covariance: float32 [8, 2, 2048, 2048], P('chan', None, 'tile')
- weights: float32 [8, 8, 2, 2048], P('chan', None, None, 'tile')
Inputs may be any that keep to these rules, and one draw needn't show every extreme that they name: `start_columns`: the 32 antenna numbers of one channel are distinct.
All inputs are finite; a program needn't handle non-finite values. No bound on the sum of `rfi_flags` on one device may be relied on, other than what follows from the above.
Results may differ from a plain program's by a relative error of at most 0.0003.
Values may be sent and summed in bfloat16 or wider, within the bound.
No kernel may reach another device: no remote copies, remote signals or barrier semaphores. Data moves between devices by JAX's collectives and lax.ppermute only.
A program may use at most 128 MiB of HBM per device.

v0:
```python
import functools
import math
import jax
import jax.numpy as jnp
from jax import lax
from jax.sharding import Mesh
from jax.sharding import PartitionSpec as P

ARRAY_ELEMENTS = 2048
SNAPSHOT_COUNT = 2048
SUB_ITERS = 4
CG_ITERS = 12
TILE = ("tile_0", "tile_1")
diagonal_loading = 0.1
highest = lax.Precision.HIGHEST


def one_axis_at_a_time(shard, axes):
    return functools.reduce(lax.psum, axes, shard)


def from_everyone(shard, axis):
    devices = lax.axis_size(axis)
    return lax.all_to_all(
        jnp.broadcast_to(shard[None], (devices, *shard.shape)), axis, 0, 0, tiled=True
    )


def laid_out(pieces, dim):
    pieces = jnp.moveaxis(pieces, 0, dim)
    dims = pieces.shape
    return pieces.reshape(*dims[:dim], dims[dim] * dims[dim + 1], *dims[dim + 2 :])


def gathered_copies(shard, axis, dim):
    pieces = from_everyone(shard, axis)
    return laid_out(pieces, dim)


def steering_table(beam_entries):
    element_index = jnp.arange(ARRAY_ELEMENTS, dtype=jnp.int32)
    steer_phases = (beam_entries[..., None] * element_index % ARRAY_ELEMENTS).astype(
        jnp.float32
    ) * (2.0 * math.pi / ARRAY_ELEMENTS)
    return jnp.stack([jnp.cos(steer_phases), jnp.sin(steer_phases)], axis=-2)


def orthonormal(vectors):
    dims_in = vectors.shape
    flattened = vectors.reshape(dims_in[:-2] + (dims_in[-2] * dims_in[-1],))
    gram_matrix = jnp.einsum("...kx,...lx->...kl", flattened, flattened, precision=highest)
    factor = jnp.linalg.cholesky(gram_matrix)
    solved = lax.linalg.triangular_solve(factor, flattened, left_side=True, lower=True)
    return solved.reshape(dims_in)


def apply_rows(covariance, vectors):
    upper_half = vectors[..., 0, :]
    lower_half = vectors[..., 1, :]
    stacked = jnp.stack(
        [jnp.stack([upper_half, -lower_half], -2), jnp.stack([lower_half, upper_half], -2)], -3
    )
    return jnp.einsum("...bhpa,...pra->...bhr", stacked, covariance, precision=highest)


def project(vectors, subspace):
    coefficients = jnp.einsum("...bha,...kha->...bk", vectors, subspace, precision=highest)
    return vectors - jnp.einsum("...bk,...kha->...bha", coefficients, subspace, precision=highest)


def shards(voltages, rfi_flags, beam_steer_index, start_columns):
    turned = lax.all_to_all(voltages, "chan", split_axis=0, concat_axis=3, tiled=True)
    tile_total_count = lax.axis_size(TILE)
    block_row_set = ARRAY_ELEMENTS // tile_total_count
    first_row = lax.axis_index(TILE) * block_row_set
    gathered = lax.all_gather(turned, TILE, axis=2, tiled=True)
    own_rows = lax.dynamic_slice_in_dim(gathered, first_row, block_row_set, 3)
    swapped = jnp.stack([own_rows[:, 1], -own_rows[:, 0]], 1)
    real_part = jnp.einsum("cpsi,cpsj->cij", own_rows, gathered, preferred_element_type=jnp.float32)
    imag_part = jnp.einsum("cpsi,cpsj->cij", swapped, gathered, preferred_element_type=jnp.float32)
    summed = jnp.stack([real_part, imag_part], 1)
    covariance = summed * (1.0 / SNAPSHOT_COUNT)
    diagonal = lax.dynamic_slice_in_dim(covariance[:, 0], first_row, block_row_set, 2)
    covariance_trace = one_axis_at_a_time(
        jnp.sum(jnp.diagonal(diagonal, axis1=1, axis2=2), axis=1), TILE
    )
    loading_amount = diagonal_loading * covariance_trace / ARRAY_ELEMENTS
    picked = jnp.take_along_axis(covariance, start_columns[:, None, None, :], axis=3)
    col_real = jnp.swapaxes(picked[:, 0], 1, 2)
    col_imag = jnp.swapaxes(picked[:, 1], 1, 2)
    rows_now = jnp.concatenate(
        [jnp.stack([col_real, col_imag], 2), jnp.stack([-col_imag, col_real], 2)], 1
    )
    for sweep_index in range(SUB_ITERS):
        full_rows = gathered_copies(rows_now, TILE, 3)
        subspace = orthonormal(full_rows)
        if sweep_index + 1 < SUB_ITERS:
            rows_now = apply_rows(covariance, subspace)
    subspace = subspace * rfi_flags.astype(jnp.float32)[:, None, None, None]
    steering = steering_table(beam_steer_index)
    load_wide = loading_amount[:, None, None, None]
    load_narrow = loading_amount[:, None]

    def cg_sweep(counter, state_tuple):
        solved_weights, residual, direction, res_norm = state_tuple
        projected = project(direction, subspace)
        mapped = gathered_copies(apply_rows(covariance, projected), TILE, 3)
        combined = project(mapped, subspace) + load_wide * direction
        curvature = jnp.sum(projected * mapped, axis=(2, 3)) + load_narrow * jnp.sum(
            direction * direction, axis=(2, 3)
        )
        step_size = res_norm / curvature
        solved_weights = solved_weights + step_size[:, :, None, None] * direction
        residual = residual - step_size[:, :, None, None] * combined
        new_norm = jnp.sum(residual * residual, axis=(2, 3))
        direction = residual + (new_norm / res_norm)[:, :, None, None] * direction
        return (solved_weights, residual, direction, new_norm)

    start_state = (
        jnp.zeros_like(steering),
        steering,
        steering,
        jnp.sum(steering * steering, axis=(2, 3)),
    )
    solved_weights = lax.fori_loop(0, CG_ITERS, cg_sweep, start_state)[0]
    array_response = jnp.sum(steering * solved_weights, axis=(2, 3))
    weights = ARRAY_ELEMENTS * solved_weights / array_response[:, :, None, None]
    shard_local_rows = lax.dynamic_slice_in_dim(weights, first_row, block_row_set, 3)
    return (covariance, shard_local_rows)


def solution(mesh):
    split = Mesh(mesh.devices.reshape(mesh.shape["chan"], 4, 4), ("chan", "tile_0", "tile_1"))
    return jax.shard_map(
        shards,
        mesh=split,
        in_specs=(P(None, None, TILE, "chan"), P("chan"), P("chan", None), P("chan", None)),
        out_specs=(P("chan", None, TILE, None), P("chan", None, None, TILE)),
        check_vma=False,
    )
```

profile of v0, /device:TPU:0, one launch (start us, length us, event | category | flops | bytes accessed | tf_op | source)
XLA Modules:
  0.0 599.7 jit_solution(14355733121557029052)
XLA Ops:
  7.2 20.4 %all_to_all.45 = bf16[8,2,128,256]{3,2,1,0:T(8,128)(2,1)S(1)} all-to-all(bf16[8,2,128,256]{3,2,1,0:T(8,128)(2,1)} %param.9), channel_id=1, replica_groups=mesh['chan'=8,'tile_0'=4,'tile_1'=4] {'chan'}, dimensions={0} | all-to-all | bytes 2097152 | tf_op jit(solution)/shard_map/all_to_all | solution.py:72
  28.8 112.0 %all-gather.2.cloned.1.call-done = bf16[1,2,2048,2048]{3,2,1,0:T(8,128)(2,1)} async-done(((bf16[1,2,128,2048]{3,2,1,0:T(8,128)(2,1)}), bf16[1,2,2048,2048]{3,2,1,0:T(8,128)(2,1)}) %all-gather.2.cloned.1.call-update) | async-done | bytes 16777232 | tf_op jit(solution)/shard_map/all_gather | solution.py:76
  140.7 8.6 %fusion.26 = f32[128,2048,1]{1,0,2:T(8,128)S(1)} fusion(bf16[1,2,2048,2048]{3,2,1,0:T(8,128)(2,1)} %all-gather.2.cloned.1.call-done, s32[]{:T(128)S(6)} %select_n.91), kind=kOutput, calls=%fused_computation.39 | convolution fusion | flops 2147483648 | bytes 18874372 | tf_op jit(solution)/shard_map/cpsi,cpsj->cij/dot_general | solution.py:79
  162.4 22.2 %all_to_all.46 = f32[16,1,64,2,128]{4,2,3,1,0:T(8,128)S(1)} all-to-all(f32[16,1,64,2,128]{4,2,3,1,0:T(8,128)S(1)} %broadcast_in_dim.49), channel_id=1, replica_groups=mesh['chan'=8,'tile_0'=4,'tile_1'=4] {'tile_0','tile_1'}, dimensions={0} | all-to-all | bytes 2097152 | tf_op jit(solution)/shard_map/all_to_all | solution.py:24
  185.7 5.8 custom-call.15
  206.6 19.4 %all_to_all.47 = f32[16,1,64,2,128]{4,2,3,1,0:T(8,128)S(1)} all-to-all(f32[16,1,64,2,128]{4,2,3,1,0:T(8,128)S(1)} %broadcast_in_dim.74), channel_id=1, replica_groups=mesh['chan'=8,'tile_0'=4,'tile_1'=4] {'tile_0','tile_1'}, dimensions={0} | all-to-all | bytes 2097152 | tf_op jit(solution)/shard_map/all_to_all | solution.py:24
  227.1 5.8 custom-call.17
  254.3 14.5 %all-to-all-done.4 = f32[16,1,64,2,128]{4,2,3,1,0:T(8,128)S(1)} async-done(((f32[16,1,64,2,128]{4,2,3,1,0:T(8,128)}), f32[16,1,64,2,128]{4,2,3,1,0:T(8,128)S(1)}, u32[]{:S(2)}, u32[]{:S(2)}) %all-to-all-start.4) | async-done | bytes 1048608 | tf_op jit(solution)/shard_map/all_to_all | solution.py:24
  269.8 5.8 custom-call.19
  300.5 11.9 %psum.14 = f32[1]{0:T(128)} all-reduce(f32[1]{0:T(128)} %bitcast.91), channel_id=1, replica_groups=mesh['chan'=8,'tile_0'=4,'tile_1'=4] {'tile_0'}, use_global_device_ids=true, to_apply=%region_4.7 | all-reduce | flops 1 | bytes 8 | tf_op jit(solution)/shard_map/psum | solution.py:19
  313.3 10.8 %psum.15 = f32[1]{0:T(128)} all-reduce(f32[1]{0:T(128)} %psum.14), channel_id=1, replica_groups=mesh['chan'=8,'tile_0'=4,'tile_1'=4] {'tile_1'}, use_global_device_ids=true, to_apply=%region_5.8 | all-reduce | flops 1 | bytes 8 | tf_op jit(solution)/shard_map/psum | solution.py:19
  343.1 246.5 %while.17 = (s32[]{:T(128)}, f32[1,8,2,2048]{3,1,2,0:T(8,128)}, f32[1,8,2,2048]{3,1,2,0:T(8,128)}, f32[1,8,2,2048]{3,1,2,0:T(8,128)S(1)}, f32[1,8]{1,0:T(1,128)S...) while((s32[]{:T(128)}, f32[1,8,2,2048]{3,1,2,0:T(8,128)}, ...), condition=%wide.region_10.13_spmd.clone, body=%wide.region_6.12_spmd.clone.sunk | while | flops 202031136 | bytes 11035319 | solution.py:125
  350.8 7.8 %all-to-all-done = f32[16,1,8,2,128]{4,2,3,1,0:T(8,128)S(1)} async-done(((f32[16,1,8,2,128]{4,2,3,1,0:T(8,128)}), f32[16,1,8,2,128]{4,2,3,1,0:T(8,128)S(1)}, u32[]{:S(2)}, u32[]{:S(2)}) %all-to-all-start) | async-done | bytes 131104 | tf_op jit(solution)/shard_map/while/body/eval_jaxpr/all_to_all | solution.py:24
  371.3 7.8 %all-to-all-done = f32[16,1,8,2,128]{4,2,3,1,0:T(8,128)S(1)} async-done(((f32[16,1,8,2,128]{4,2,3,1,0:T(8,128)}), f32[16,1,8,2,128]{4,2,3,1,0:T(8,128)S(1)}, u32[]{:S(2)}, u32[]{:S(2)}) %all-to-all-start) | async-done | bytes 131104 | tf_op jit(solution)/shard_map/while/body/eval_jaxpr/all_to_all | solution.py:24
  391.9 7.8 %all-to-all-done = f32[16,1,8,2,128]{4,2,3,1,0:T(8,128)S(1)} async-done(((f32[16,1,8,2,128]{4,2,3,1,0:T(8,128)}), f32[16,1,8,2,128]{4,2,3,1,0:T(8,128)S(1)}, u32[]{:S(2)}, u32[]{:S(2)}) %all-to-all-start) | async-done | bytes 131104 | tf_op jit(solution)/shard_map/while/body/eval_jaxpr/all_to_all | solution.py:24
  412.4 7.8 %all-to-all-done = f32[16,1,8,2,128]{4,2,3,1,0:T(8,128)S(1)} async-done(((f32[16,1,8,2,128]{4,2,3,1,0:T(8,128)}), f32[16,1,8,2,128]{4,2,3,1,0:T(8,128)S(1)}, u32[]{:S(2)}, u32[]{:S(2)}) %all-to-all-start) | async-done | bytes 131104 | tf_op jit(solution)/shard_map/while/body/eval_jaxpr/all_to_all | solution.py:24
  432.9 7.8 %all-to-all-done = f32[16,1,8,2,128]{4,2,3,1,0:T(8,128)S(1)} async-done(((f32[16,1,8,2,128]{4,2,3,1,0:T(8,128)}), f32[16,1,8,2,128]{4,2,3,1,0:T(8,128)S(1)}, u32[]{:S(2)}, u32[]{:S(2)}) %all-to-all-start) | async-done | bytes 131104 | tf_op jit(solution)/shard_map/while/body/eval_jaxpr/all_to_all | solution.py:24
  453.5 7.8 %all-to-all-done = f32[16,1,8,2,128]{4,2,3,1,0:T(8,128)S(1)} async-done(((f32[16,1,8,2,128]{4,2,3,1,0:T(8,128)}), f32[16,1,8,2,128]{4,2,3,1,0:T(8,128)S(1)}, u32[]{:S(2)}, u32[]{:S(2)}) %all-to-all-start) | async-done | bytes 131104 | tf_op jit(solution)/shard_map/while/body/eval_jaxpr/all_to_all | solution.py:24
  474.0 7.8 %all-to-all-done = f32[16,1,8,2,128]{4,2,3,1,0:T(8,128)S(1)} async-done(((f32[16,1,8,2,128]{4,2,3,1,0:T(8,128)}), f32[16,1,8,2,128]{4,2,3,1,0:T(8,128)S(1)}, u32[]{:S(2)}, u32[]{:S(2)}) %all-to-all-start) | async-done | bytes 131104 | tf_op jit(solution)/shard_map/while/body/eval_jaxpr/all_to_all | solution.py:24
  494.6 7.8 %all-to-all-done = f32[16,1,8,2,128]{4,2,3,1,0:T(8,128)S(1)} async-done(((f32[16,1,8,2,128]{4,2,3,1,0:T(8,128)}), f32[16,1,8,2,128]{4,2,3,1,0:T(8,128)S(1)}, u32[]{:S(2)}, u32[]{:S(2)}) %all-to-all-start) | async-done | bytes 131104 | tf_op jit(solution)/shard_map/while/body/eval_jaxpr/all_to_all | solution.py:24
  515.1 7.8 %all-to-all-done = f32[16,1,8,2,128]{4,2,3,1,0:T(8,128)S(1)} async-done(((f32[16,1,8,2,128]{4,2,3,1,0:T(8,128)}), f32[16,1,8,2,128]{4,2,3,1,0:T(8,128)S(1)}, u32[]{:S(2)}, u32[]{:S(2)}) %all-to-all-start) | async-done | bytes 131104 | tf_op jit(solution)/shard_map/while/body/eval_jaxpr/all_to_all | solution.py:24
  535.6 7.8 %all-to-all-done = f32[16,1,8,2,128]{4,2,3,1,0:T(8,128)S(1)} async-done(((f32[16,1,8,2,128]{4,2,3,1,0:T(8,128)}), f32[16,1,8,2,128]{4,2,3,1,0:T(8,128)S(1)}, u32[]{:S(2)}, u32[]{:S(2)}) %all-to-all-start) | async-done | bytes 131104 | tf_op jit(solution)/shard_map/while/body/eval_jaxpr/all_to_all | solution.py:24
  556.2 7.8 %all-to-all-done = f32[16,1,8,2,128]{4,2,3,1,0:T(8,128)S(1)} async-done(((f32[16,1,8,2,128]{4,2,3,1,0:T(8,128)}), f32[16,1,8,2,128]{4,2,3,1,0:T(8,128)S(1)}, u32[]{:S(2)}, u32[]{:S(2)}) %all-to-all-start) | async-done | bytes 131104 | tf_op jit(solution)/shard_map/while/body/eval_jaxpr/all_to_all | solution.py:24
  576.7 7.8 %all-to-all-done = f32[16,1,8,2,128]{4,2,3,1,0:T(8,128)S(1)} async-done(((f32[16,1,8,2,128]{4,2,3,1,0:T(8,128)}), f32[16,1,8,2,128]{4,2,3,1,0:T(8,128)S(1)}, u32[]{:S(2)}, u32[]{:S(2)}) %all-to-all-start) | async-done | bytes 131104 | tf_op jit(solution)/shard_map/while/body/eval_jaxpr/all_to_all | solution.py:24
  (339 shorter events, 251.9 us)
Async XLA Ops:
  7.2 133.6 %all-gather.2.cloned.1.call-start = ((), (), s32[]{:S(2)}) async-start(), calls=%async_computation.6 | async-start | bytes 17825792 | tf_op jit(solution)/shard_map/all_gather | solution.py:76
  140.7 10.9 %copy-start = (bf16[1,2,2048,2048]{3,2,1,0:T(8,128)(2,1)S(1)}, bf16[1,2,2048,2048]{3,2,1,0:T(8,128)(2,1)}, u32[]{:S(2)}) copy-start(bf16[1,2,2048,2048]{3,2,1,0:T(8,128)(2,1)} %all-gather.2.cloned.1.call-done) | copy-start | bytes 50331652
  151.6 137.1 %copy-start.2 = (f32[128,2048,1]{1,0,2:T(8,128)}, f32[128,2048,1]{1,0,2:T(8,128)S(1)}, u32[]{:S(2)}) copy-start(f32[128,2048,1]{1,0,2:T(8,128)S(1)} %fusion.26) | copy-start | bytes 3145732
  247.9 5.8 copy-start.7
  249.0 19.7 %all-to-all-start.4 = ((f32[16,1,64,2,128]{4,2,3,1,0:T(8,128)}), f32[16,1,64,2,128]{4,2,3,1,0:T(8,128)S(1)}, u32[]{:S(2)}, u32[]{:S(2)}) async-start(f32[16,1,64,2,128]{4,2,3,1,0:T(8,128)} %broadcast_in_dim.75), calls=%async_computation.4 | async-start | bytes 2097152 | tf_op jit(solution)/shard_map/all_to_all | solution.py:24
  291.7 33.1 %all-to-all-start.5 = ((f32[16,1,64,2,128]{4,2,3,1,0:T(8,128)}), f32[16,1,64,2,128]{4,2,3,1,0:T(8,128)}, u32[]{:S(2)}, u32[]{:S(2)}) async-start(f32[16,1,64,2,128]{4,2,3,1,0:T(8,128)} %broadcast_in_dim.76), calls=%async_computation.5 | async-start | bytes 2097152 | tf_op jit(solution)/shard_map/all_to_all | solution.py:24
  347.1 11.5 %all-to-all-start = ((f32[16,1,8,2,128]{4,2,3,1,0:T(8,128)}), f32[16,1,8,2,128]{4,2,3,1,0:T(8,128)S(1)}, u32[]{:S(2)}, u32[]{:S(2)}) async-start(f32[16,1,8,2,128]{4,2,3,1,0:T(8,128)} %broadcast_in_dim.83), calls=%async_computation | async-start | bytes 262144 | tf_op jit(solution)/shard_map/while/body/eval_jaxpr/all_to_all | solution.py:24
  358.6 3.4 copy-start.3
  367.7 11.5 %all-to-all-start = ((f32[16,1,8,2,128]{4,2,3,1,0:T(8,128)}), f32[16,1,8,2,128]{4,2,3,1,0:T(8,128)S(1)}, u32[]{:S(2)}, u32[]{:S(2)}) async-start(f32[16,1,8,2,128]{4,2,3,1,0:T(8,128)} %broadcast_in_dim.83), calls=%async_computation | async-start | bytes 262144 | tf_op jit(solution)/shard_map/while/body/eval_jaxpr/all_to_all | solution.py:24
  379.1 3.4 copy-start.3
  388.2 11.5 %all-to-all-start = ((f32[16,1,8,2,128]{4,2,3,1,0:T(8,128)}), f32[16,1,8,2,128]{4,2,3,1,0:T(8,128)S(1)}, u32[]{:S(2)}, u32[]{:S(2)}) async-start(f32[16,1,8,2,128]{4,2,3,1,0:T(8,128)} %broadcast_in_dim.83), calls=%async_computation | async-start | bytes 262144 | tf_op jit(solution)/shard_map/while/body/eval_jaxpr/all_to_all | solution.py:24
  399.7 3.4 copy-start.3
  408.7 11.5 %all-to-all-start = ((f32[16,1,8,2,128]{4,2,3,1,0:T(8,128)}), f32[16,1,8,2,128]{4,2,3,1,0:T(8,128)S(1)}, u32[]{:S(2)}, u32[]{:S(2)}) async-start(f32[16,1,8,2,128]{4,2,3,1,0:T(8,128)} %broadcast_in_dim.83), calls=%async_computation | async-start | bytes 262144 | tf_op jit(solution)/shard_map/while/body/eval_jaxpr/all_to_all | solution.py:24
  420.2 3.4 copy-start.3
  429.3 11.5 %all-to-all-start = ((f32[16,1,8,2,128]{4,2,3,1,0:T(8,128)}), f32[16,1,8,2,128]{4,2,3,1,0:T(8,128)S(1)}, u32[]{:S(2)}, u32[]{:S(2)}) async-start(f32[16,1,8,2,128]{4,2,3,1,0:T(8,128)} %broadcast_in_dim.83), calls=%async_computation | async-start | bytes 262144 | tf_op jit(solution)/shard_map/while/body/eval_jaxpr/all_to_all | solution.py:24
  449.8 11.5 %all-to-all-start = ((f32[16,1,8,2,128]{4,2,3,1,0:T(8,128)}), f32[16,1,8,2,128]{4,2,3,1,0:T(8,128)S(1)}, u32[]{:S(2)}, u32[]{:S(2)}) async-start(f32[16,1,8,2,128]{4,2,3,1,0:T(8,128)} %broadcast_in_dim.83), calls=%async_computation | async-start | bytes 262144 | tf_op jit(solution)/shard_map/while/body/eval_jaxpr/all_to_all | solution.py:24
  461.3 3.4 copy-start.3
  470.4 11.5 %all-to-all-start = ((f32[16,1,8,2,128]{4,2,3,1,0:T(8,128)}), f32[16,1,8,2,128]{4,2,3,1,0:T(8,128)S(1)}, u32[]{:S(2)}, u32[]{:S(2)}) async-start(f32[16,1,8,2,128]{4,2,3,1,0:T(8,128)} %broadcast_in_dim.83), calls=%async_computation | async-start | bytes 262144 | tf_op jit(solution)/shard_map/while/body/eval_jaxpr/all_to_all | solution.py:24
  490.9 11.5 %all-to-all-start = ((f32[16,1,8,2,128]{4,2,3,1,0:T(8,128)}), f32[16,1,8,2,128]{4,2,3,1,0:T(8,128)S(1)}, u32[]{:S(2)}, u32[]{:S(2)}) async-start(f32[16,1,8,2,128]{4,2,3,1,0:T(8,128)} %broadcast_in_dim.83), calls=%async_computation | async-start | bytes 262144 | tf_op jit(solution)/shard_map/while/body/eval_jaxpr/all_to_all | solution.py:24
  511.4 11.5 %all-to-all-start = ((f32[16,1,8,2,128]{4,2,3,1,0:T(8,128)}), f32[16,1,8,2,128]{4,2,3,1,0:T(8,128)S(1)}, u32[]{:S(2)}, u32[]{:S(2)}) async-start(f32[16,1,8,2,128]{4,2,3,1,0:T(8,128)} %broadcast_in_dim.83), calls=%async_computation | async-start | bytes 262144 | tf_op jit(solution)/shard_map/while/body/eval_jaxpr/all_to_all | solution.py:24
  522.9 3.4 copy-start.3
  532.0 11.5 %all-to-all-start = ((f32[16,1,8,2,128]{4,2,3,1,0:T(8,128)}), f32[16,1,8,2,128]{4,2,3,1,0:T(8,128)S(1)}, u32[]{:S(2)}, u32[]{:S(2)}) async-start(f32[16,1,8,2,128]{4,2,3,1,0:T(8,128)} %broadcast_in_dim.83), calls=%async_computation | async-start | bytes 262144 | tf_op jit(solution)/shard_map/while/body/eval_jaxpr/all_to_all | solution.py:24
  552.5 11.5 %all-to-all-start = ((f32[16,1,8,2,128]{4,2,3,1,0:T(8,128)}), f32[16,1,8,2,128]{4,2,3,1,0:T(8,128)S(1)}, u32[]{:S(2)}, u32[]{:S(2)}) async-start(f32[16,1,8,2,128]{4,2,3,1,0:T(8,128)} %broadcast_in_dim.83), calls=%async_computation | async-start | bytes 262144 | tf_op jit(solution)/shard_map/while/body/eval_jaxpr/all_to_all | solution.py:24
  573.0 11.5 %all-to-all-start = ((f32[16,1,8,2,128]{4,2,3,1,0:T(8,128)}), f32[16,1,8,2,128]{4,2,3,1,0:T(8,128)S(1)}, u32[]{:S(2)}, u32[]{:S(2)}) async-start(f32[16,1,8,2,128]{4,2,3,1,0:T(8,128)} %broadcast_in_dim.83), calls=%async_computation | async-start | bytes 262144 | tf_op jit(solution)/shard_map/while/body/eval_jaxpr/all_to_all | solution.py:24
  (22 other events, 35.1 us)
Sparse Core Ops, SparseCore 0:
  28.9 111.8 all-gather.1
where the time goes:
time: 607 us; the launch traced here: 600 us
  waiting for transfers between devices  220 us (36%)
  matrix products  109 us (18%)
  blocking collectives  84.7 us (14%)
  other arithmetic  73.4 us (12%)
  starting transfers between devices  50.6 us (8%)
  local copies, waits for them, and re-layouts  45 us (7%)
  between operations  16 us (3%)
    all_gather x1, waiting for transfers between devices, shards(): gathered = lax.all_gather(turned, TILE, axis=2, tiled=True)  112 us
    all_to_all x14, waiting for transfers between devices, from_everyone(): lax.all_to_all(jnp.broadcast_to(shard[None], (devices, *shard.shape)), ax...  108 us
    all_to_all x14, starting transfers between devices, from_everyone(): lax.all_to_all(jnp.broadcast_to(shard[None], (devices, *shard.shape)), ax...  50.6 us
    all_to_all x2, blocking collectives, from_everyone(): lax.all_to_all(jnp.broadcast_to(shard[None], (devices, *shard.shape)), ax...  41.7 us
    dot_general x24, matrix products, project(): jnp.einsum('...bk,...kha->...bha', coefficients, subspace, precision=high...  35 us
    dot_general x15, matrix products, apply_rows(): jnp.einsum('...bhpa,...pra->...bhr', stacked, covariance, precision=highest)  26.4 us
    another operation x12, other arithmetic, orthonormal(): factor = jnp.linalg.cholesky(gram_matrix)  26.1 us
    psum x2, blocking collectives, one_axis_at_a_time(): return functools.reduce(lax.psum, axes, shard)  22.7 us
  transfers between devices with their start and end apart: 15, of which 14 were waited for; matrix products, arithmetic and copies ran while one was open for 1% of the time, Pallas kernels for 0%

commit v1 on v0

--- a/solution.py
+++ b/solution.py
@@ -73,7 +73,9 @@
     tile_total_count = lax.axis_size(TILE)
     block_row_set = ARRAY_ELEMENTS // tile_total_count
     first_row = lax.axis_index(TILE) * block_row_set
-    gathered = lax.all_gather(turned, TILE, axis=2, tiled=True)
+    arr_now = jnp.stack([turned for _ in range(lax.psum(1, axis_name=TILE))], axis=0)
+    moved = lax.all_to_all(arr_now, TILE, 0, 0)
+    gathered = jnp.concatenate(moved, axis=2)
     own_rows = lax.dynamic_slice_in_dim(gathered, first_row, block_row_set, 3)
     swapped = jnp.stack([own_rows[:, 1], -own_rows[:, 0]], 1)
     real_part = jnp.einsum("cpsi,cpsj->cij", own_rows, gathered, preferred_element_type=jnp.float32)

time: 607 us -> 812 us (1.34)
  waiting for transfers between devices: 220 us -> 356 us
  local copies, waits for them, and re-layouts: 45 us -> 113 us
  between operations: 16 us -> 2.76 us
  starting transfers between devices: 50.6 us -> 58.8 us
    all_to_all x0 -> x1, waiting for transfers between devices: none -> 248 us  [shards(): moved = lax.all_to_all(arr_now, TILE, 0, 0)]
    all_gather x1 -> x0, waiting for transfers between devices: 112 us -> none  [shards(): gathered = lax.all_gather(turned, TILE, axis=2, tiled=True)]
    reshape x0 -> x3, local copies, waits for them, and re-layouts: none -> 63.1 us  [shards(): gathered = jnp.concatenate(moved, axis=2)]
    all_to_all x0 -> x1, starting transfers between devices: none -> 8.23 us  [shards(): moved = lax.all_to_all(arr_now, TILE, 0, 0)]
where the time goes in v1:
time: 812 us; the launch traced here: 802 us
  waiting for transfers between devices  356 us (44%)
  matrix products  116 us (14%)
  local copies, waits for them, and re-layouts  113 us (14%)
  blocking collectives  81.6 us (10%)
  other arithmetic  73.7 us (9%)
  starting transfers between devices  58.8 us (7%)
    all_to_all x1, waiting for transfers between devices, shards(): moved = lax.all_to_all(arr_now, TILE, 0, 0)  248 us
    all_to_all x14, waiting for transfers between devices, from_everyone(): lax.all_to_all(jnp.broadcast_to(shard[None], (devices, *shard.shape)), ax...  108 us
    reshape x3, local copies, waits for them, and re-layouts, shards(): gathered = jnp.concatenate(moved, axis=2)  63.1 us
    all_to_all x14, starting transfers between devices, from_everyone(): lax.all_to_all(jnp.broadcast_to(shard[None], (devices, *shard.shape)), ax...  50.6 us
    all_to_all x2, blocking collectives, from_everyone(): lax.all_to_all(jnp.broadcast_to(shard[None], (devices, *shard.shape)), ax...  38.8 us
    dot_general x24, matrix products, project(): jnp.einsum('...bk,...kha->...bha', coefficients, subspace, precision=high...  35 us
    dot_general x15, matrix products, apply_rows(): jnp.einsum('...bhpa,...pra->...bhr', stacked, covariance, precision=highest)  26.4 us
    another operation x12, other arithmetic, orthonormal(): factor = jnp.linalg.cholesky(gram_matrix)  26.1 us
  transfers between devices with their start and end apart: 15, of which 14 were waited for; matrix products, arithmetic and copies ran while one was open for 1% of the time, Pallas kernels for 0%

profile of v1, /device:TPU:0, one launch (start us, length us, event | category | flops | bytes accessed | tf_op | source)
XLA Modules:
  0.0 802.4 jit_solution(17353037750736723979)
XLA Ops:
  2.3 20.2 %all_to_all.47 = bf16[8,2,128,256]{2,3,1,0:T(8,128)(2,1)S(1)} all-to-all(bf16[8,2,128,256]{2,3,1,0:T(8,128)(2,1)S(1)} %copy.84), channel_id=1, replica_groups=mesh['chan'=8,'tile_0'=4,'tile_1'=4] {'chan'}, dimensions={0} | all-to-all | bytes 2097152 | tf_op jit(solution)/shard_map/all_to_all | solution.py:72
  29.1 8.2 %all-to-all-start.2 = ((bf16[16,1,2,128,2048]{4,3,2,1,0:T(8,128)(2,1)}), bf16[16,1,2,128,2048]{4,3,2,1,0:T(8,128)(2,1)}, u32[]{:S(2)}, u32[]{:S(2)}) async-start(bf16[16,1,2,128,2048]{4,3,2,1,0:T(8,128)(2,1)} %stack.132), calls=%async_computation.2 | async-start | bytes 33554432 | tf_op jit(solution)/shard_map/all_to_all | solution.py:77
  37.4 247.9 %all-to-all-done.2 = bf16[16,1,2,128,2048]{4,3,2,1,0:T(8,128)(2,1)} async-done(((bf16[16,1,2,128,2048]{4,3,2,1,0:T(8,128)(2,1)}), bf16[16,1,2,128,2048]{4,3,2,1,0:T(8,128)(2,1)}, u32[]{:S(2)}, u32[]{:S(2)}) %all-to-all-start.2) | async-done | bytes 16777248 | tf_op jit(solution)/shard_map/all_to_all | solution.py:77
  285.3 14.1 %copy.88 = bf16[1,2,16,128,2048]{4,3,2,1,0:T(8,128)(2,1)} copy(bf16[1,2,16,128,2048]{4,3,1,0,2:T(8,128)(2,1)} %bitcast.3) | data formatting | bytes 33554432 | tf_op jit(solution)/shard_map/reshape | solution.py:78
  299.4 23.7 %copy.87 = bf16[1,2,16,128,2048]{3,2,4,1,0:T(8,128)(2,1)} copy(bf16[1,2,16,128,2048]{4,3,1,0,2:T(8,128)(2,1)} %bitcast.3) | data formatting | bytes 33554432 | tf_op jit(solution)/shard_map/reshape | solution.py:78
  323.1 25.3 %reshape.671 = bf16[1,2,2048,2048]{2,3,1,0:T(8,128)(2,1)} reshape(bf16[1,2,16,128,2048]{3,2,4,1,0:T(8,128)(2,1)} %copy.87) | data formatting | bytes 33554432 | tf_op jit(solution)/shard_map/reshape | solution.py:78
  349.8 8.4 %fusion.60 = f32[128,2048,1]{1,0,2:T(8,128)S(1)} fusion(bf16[2,2048,2048]{2,1,0:T(8,128)(2,1)} %bitcast.343, bf16[1,2,2048,2048]{2,3,1,0:T(8,128)(2,1)} %reshape.671, s32[]{:T(128)S(6)} %select_n.91), kind=kOutput, calls=%fused_computation.87 | convolution fusion | flops 2147483648 | bytes 18874372 | tf_op jit(solution)/shard_map/cpsi,cpsj->cij/dot_general | solution.py:81
  358.2 8.1 %fusion.41 = f32[128,2048,1]{1,0,2:T(8,128)S(1)} fusion(bf16[2,2048,2048]{2,1,0:T(8,128)(2,1)} %bitcast.344, bf16[1,1,2048,128]{2,3,1,0:T(8,128)(2,1)S(1)} %get-tuple-element.146, bf16[1,1,2048,128]{2,3,1,0:T(8,128)(2,1)S(1)} %get-tuple-element.145), kind=kOutput, calls=%fused_computation.62 | convolution fusion | flops 2148007936 | bytes 18874368 | tf_op jit(solution)/shard_map/cpsi,cpsj->cij/dot_general | solution.py:82
  374.6 20.6 %all_to_all.48 = f32[16,1,64,2,128]{4,2,3,1,0:T(8,128)S(1)} all-to-all(f32[16,1,64,2,128]{4,2,3,1,0:T(8,128)S(1)} %broadcast_in_dim.49), channel_id=1, replica_groups=mesh['chan'=8,'tile_0'=4,'tile_1'=4] {'tile_0','tile_1'}, dimensions={0} | all-to-all | bytes 2097152 | tf_op jit(solution)/shard_map/all_to_all | solution.py:24
  417.2 18.2 %all_to_all.49 = f32[16,1,64,2,128]{4,2,3,1,0:T(8,128)S(1)} all-to-all(f32[16,1,64,2,128]{4,2,3,1,0:T(8,128)S(1)} %broadcast_in_dim.74), channel_id=1, replica_groups=mesh['chan'=8,'tile_0'=4,'tile_1'=4] {'tile_0','tile_1'}, dimensions={0} | all-to-all | bytes 2097152 | tf_op jit(solution)/shard_map/all_to_all | solution.py:24
  462.9 14.0 %all-to-all-done.5 = f32[16,1,64,2,128]{4,2,3,1,0:T(8,128)S(1)} async-done(((f32[16,1,64,2,128]{4,2,3,1,0:T(8,128)}), f32[16,1,64,2,128]{4,2,3,1,0:T(8,128)S(1)}, u32[]{:S(2)}, u32[]{:S(2)}) %all-to-all-start.5) | async-done | bytes 1048608 | tf_op jit(solution)/shard_map/all_to_all | solution.py:24
  511.1 11.4 %psum.14 = f32[1]{0:T(128)} all-reduce(f32[1]{0:T(128)} %bitcast.93), channel_id=1, replica_groups=mesh['chan'=8,'tile_0'=4,'tile_1'=4] {'tile_0'}, use_global_device_ids=true, to_apply=%region_4.7 | all-reduce | flops 1 | bytes 8 | tf_op jit(solution)/shard_map/psum | solution.py:19
  522.5 11.3 %psum.15 = f32[1]{0:T(128)} all-reduce(f32[1]{0:T(128)} %psum.14), channel_id=1, replica_groups=mesh['chan'=8,'tile_0'=4,'tile_1'=4] {'tile_1'}, use_global_device_ids=true, to_apply=%region_5.8 | all-reduce | flops 1 | bytes 8 | tf_op jit(solution)/shard_map/psum | solution.py:19
  552.8 246.5 %while.17 = (s32[]{:T(128)}, f32[1,8,2,2048]{3,1,2,0:T(8,128)}, f32[1,8,2,2048]{3,1,2,0:T(8,128)}, f32[1,8,2,2048]{3,1,2,0:T(8,128)S(1)}, f32[1,8]{1,0:T(1,128)S...) while((s32[]{:T(128)}, f32[1,8,2,2048]{3,1,2,0:T(8,128)}, ...), condition=%wide.region_10.13_spmd.clone, body=%wide.region_6.12_spmd.clone.sunk | while | flops 202031136 | bytes 11035327 | solution.py:127
  560.5 7.8 all-to-all-done
  581.0 7.8 all-to-all-done
  601.5 7.8 all-to-all-done
  622.1 7.8 all-to-all-done
  642.6 7.8 all-to-all-done
  663.2 7.8 all-to-all-done
  683.7 7.8 all-to-all-done
  704.2 7.8 all-to-all-done
  745.3 7.8 all-to-all-done
  765.9 7.8 all-to-all-done
  (344 shorter events, 289.2 us)
Async XLA Ops:
  29.1 8.2 %copy-start.8 = (s32[1,32]{1,0:T(1,128)S(1)}, s32[1,32]{1,0:T(1,128)}, u32[]{:S(2)}) copy-start(s32[1,32]{1,0:T(1,128)} %param.12) | copy-start | bytes 388
  29.1 256.2 %all-to-all-start.2 = ((bf16[16,1,2,128,2048]{4,3,2,1,0:T(8,128)(2,1)}), bf16[16,1,2,128,2048]{4,3,2,1,0:T(8,128)(2,1)}, u32[]{:S(2)}, u32[]{:S(2)}) async-start(bf16[16,1,2,128,2048]{4,3,2,1,0:T(8,128)(2,1)} %stack.132), calls=%async_computation.2 | async-start | bytes 33554432 | tf_op jit(solution)/shard_map/all_to_all | solution.py:77
  366.4 132.7 %copy-start.1 = (f32[128,2048,1]{1,0,2:T(8,128)}, f32[128,2048,1]{1,0,2:T(8,128)S(1)}, u32[]{:S(2)}) copy-start(f32[128,2048,1]{1,0,2:T(8,128)S(1)} %fusion.41) | copy-start | bytes 3145732
  457.3 5.2 copy-start.7
  458.4 18.5 %all-to-all-start.5 = ((f32[16,1,64,2,128]{4,2,3,1,0:T(8,128)}), f32[16,1,64,2,128]{4,2,3,1,0:T(8,128)S(1)}, u32[]{:S(2)}, u32[]{:S(2)}) async-start(f32[16,1,64,2,128]{4,2,3,1,0:T(8,128)} %broadcast_in_dim.75), calls=%async_computation.5 | async-start | bytes 2097152 | tf_op jit(solution)/shard_map/all_to_all | solution.py:24
  462.8 43.6 %copy-start.5 = (f32[1,8,1,2048]{3,1,2,0:T(8,128)}, f32[1,8,1,2048]{3,1,2,0:T(8,128)S(1)}, u32[]{:S(2)}) copy-start(f32[1,8,1,2048]{3,1,2,0:T(8,128)S(1)} %get-tuple-element.169) | copy-start | bytes 196612
  462.9 43.6 %copy-start.6 = (f32[1,8,1,2048]{3,1,2,0:T(8,128)}, f32[1,8,1,2048]{3,1,2,0:T(8,128)S(1)}, u32[]{:S(2)}) copy-start(f32[1,8,1,2048]{3,1,2,0:T(8,128)S(1)} %get-tuple-element.170) | copy-start | bytes 196612
  502.1 32.3 %all-to-all-start.6 = ((f32[16,1,64,2,128]{4,2,3,1,0:T(8,128)}), f32[16,1,64,2,128]{4,2,3,1,0:T(8,128)}, u32[]{:S(2)}, u32[]{:S(2)}) async-start(f32[16,1,64,2,128]{4,2,3,1,0:T(8,128)} %broadcast_in_dim.76), calls=%async_computation.6 | async-start | bytes 2097152 | tf_op jit(solution)/shard_map/all_to_all | solution.py:24
  556.8 11.5 %all-to-all-start = ((f32[16,1,8,2,128]{4,2,3,1,0:T(8,128)}), f32[16,1,8,2,128]{4,2,3,1,0:T(8,128)S(1)}, u32[]{:S(2)}, u32[]{:S(2)}) async-start(f32[16,1,8,2,128]{4,2,3,1,0:T(8,128)} %broadcast_in_dim.83), calls=%async_computation | async-start | bytes 262144 | tf_op jit(solution)/shard_map/while/body/eval_jaxpr/all_to_all | solution.py:24
  568.3 3.4 copy-start.3
  577.3 11.5 %all-to-all-start = ((f32[16,1,8,2,128]{4,2,3,1,0:T(8,128)}), f32[16,1,8,2,128]{4,2,3,1,0:T(8,128)S(1)}, u32[]{:S(2)}, u32[]{:S(2)}) async-start(f32[16,1,8,2,128]{4,2,3,1,0:T(8,128)} %broadcast_in_dim.83), calls=%async_computation | async-start | bytes 262144 | tf_op jit(solution)/shard_map/while/body/eval_jaxpr/all_to_all | solution.py:24
  588.8 3.4 copy-start.3
  597.9 11.5 %all-to-all-start = ((f32[16,1,8,2,128]{4,2,3,1,0:T(8,128)}), f32[16,1,8,2,128]{4,2,3,1,0:T(8,128)S(1)}, u32[]{:S(2)}, u32[]{:S(2)}) async-start(f32[16,1,8,2,128]{4,2,3,1,0:T(8,128)} %broadcast_in_dim.83), calls=%async_computation | async-start | bytes 262144 | tf_op jit(solution)/shard_map/while/body/eval_jaxpr/all_to_all | solution.py:24
  609.3 3.4 copy-start.3
  618.4 11.5 %all-to-all-start = ((f32[16,1,8,2,128]{4,2,3,1,0:T(8,128)}), f32[16,1,8,2,128]{4,2,3,1,0:T(8,128)S(1)}, u32[]{:S(2)}, u32[]{:S(2)}) async-start(f32[16,1,8,2,128]{4,2,3,1,0:T(8,128)} %broadcast_in_dim.83), calls=%async_computation | async-start | bytes 262144 | tf_op jit(solution)/shard_map/while/body/eval_jaxpr/all_to_all | solution.py:24
  639.0 11.5 %all-to-all-start = ((f32[16,1,8,2,128]{4,2,3,1,0:T(8,128)}), f32[16,1,8,2,128]{4,2,3,1,0:T(8,128)S(1)}, u32[]{:S(2)}, u32[]{:S(2)}) async-start(f32[16,1,8,2,128]{4,2,3,1,0:T(8,128)} %broadcast_in_dim.83), calls=%async_computation | async-start | bytes 262144 | tf_op jit(solution)/shard_map/while/body/eval_jaxpr/all_to_all | solution.py:24
  659.5 11.5 %all-to-all-start = ((f32[16,1,8,2,128]{4,2,3,1,0:T(8,128)}), f32[16,1,8,2,128]{4,2,3,1,0:T(8,128)S(1)}, u32[]{:S(2)}, u32[]{:S(2)}) async-start(f32[16,1,8,2,128]{4,2,3,1,0:T(8,128)} %broadcast_in_dim.83), calls=%async_computation | async-start | bytes 262144 | tf_op jit(solution)/shard_map/while/body/eval_jaxpr/all_to_all | solution.py:24
  680.0 11.5 %all-to-all-start = ((f32[16,1,8,2,128]{4,2,3,1,0:T(8,128)}), f32[16,1,8,2,128]{4,2,3,1,0:T(8,128)S(1)}, u32[]{:S(2)}, u32[]{:S(2)}) async-start(f32[16,1,8,2,128]{4,2,3,1,0:T(8,128)} %broadcast_in_dim.83), calls=%async_computation | async-start | bytes 262144 | tf_op jit(solution)/shard_map/while/body/eval_jaxpr/all_to_all | solution.py:24
  700.6 11.5 %all-to-all-start = ((f32[16,1,8,2,128]{4,2,3,1,0:T(8,128)}), f32[16,1,8,2,128]{4,2,3,1,0:T(8,128)S(1)}, u32[]{:S(2)}, u32[]{:S(2)}) async-start(f32[16,1,8,2,128]{4,2,3,1,0:T(8,128)} %broadcast_in_dim.83), calls=%async_computation | async-start | bytes 262144 | tf_op jit(solution)/shard_map/while/body/eval_jaxpr/all_to_all | solution.py:24
  721.1 11.5 %all-to-all-start = ((f32[16,1,8,2,128]{4,2,3,1,0:T(8,128)}), f32[16,1,8,2,128]{4,2,3,1,0:T(8,128)S(1)}, u32[]{:S(2)}, u32[]{:S(2)}) async-start(f32[16,1,8,2,128]{4,2,3,1,0:T(8,128)} %broadcast_in_dim.83), calls=%async_computation | async-start | bytes 262144 | tf_op jit(solution)/shard_map/while/body/eval_jaxpr/all_to_all | solution.py:24
  741.6 11.5 %all-to-all-start = ((f32[16,1,8,2,128]{4,2,3,1,0:T(8,128)}), f32[16,1,8,2,128]{4,2,3,1,0:T(8,128)S(1)}, u32[]{:S(2)}, u32[]{:S(2)}) async-start(f32[16,1,8,2,128]{4,2,3,1,0:T(8,128)} %broadcast_in_dim.83), calls=%async_computation | async-start | bytes 262144 | tf_op jit(solution)/shard_map/while/body/eval_jaxpr/all_to_all | solution.py:24
  753.1 3.4 copy-start.3
  762.2 11.5 %all-to-all-start = ((f32[16,1,8,2,128]{4,2,3,1,0:T(8,128)}), f32[16,1,8,2,128]{4,2,3,1,0:T(8,128)S(1)}, u32[]{:S(2)}, u32[]{:S(2)}) async-start(f32[16,1,8,2,128]{4,2,3,1,0:T(8,128)} %broadcast_in_dim.83), calls=%async_computation | async-start | bytes 262144 | tf_op jit(solution)/shard_map/while/body/eval_jaxpr/all_to_all | solution.py:24
  782.7 11.5 %all-to-all-start = ((f32[16,1,8,2,128]{4,2,3,1,0:T(8,128)}), f32[16,1,8,2,128]{4,2,3,1,0:T(8,128)S(1)}, u32[]{:S(2)}, u32[]{:S(2)}) async-start(f32[16,1,8,2,128]{4,2,3,1,0:T(8,128)} %broadcast_in_dim.83), calls=%async_computation | async-start | bytes 262144 | tf_op jit(solution)/shard_map/while/body/eval_jaxpr/all_to_all | solution.py:24
  (22 other events, 39.0 us)
